TPU v7x, 32 devices: a whole 2x2x4 slice. The times are simulated.
32 devices in a mesh: district: 4 (over y, core), sub: 8 (over z, x).
Axes of the slice: x: 2, y: 2, z: 4, core: 2. Of those that a mesh axis runs over, the one named last changes fastest.
Arguments:
- cost_terms: bfloat16 [8, 512, 768], P('district', 'sub'), may hold values from -6 to 6
- neighbours: int32 [8, 512, 4], P('district', 'sub'), may hold values from 0 to 511, as said below
- relayout: int32 [8, 512], P('district'), may hold values from 0 to 511, as said below
- ownership: int32 [8, 512], P('district', 'sub'), may hold values from 0 to 31
- capacity: float32 [16, 48], replicated, may hold values from -67.88225 to 67.88225
- coupling: bfloat16 [8, 768, 192], P('district'), may hold values from -0.21875 to 0.21875
- solve_factor: bfloat16 [8, 768, 768], P('district')
Outputs:
- control_plan: float32 [8, 512, 768], P('district', 'sub')
- flow_prices: float32 [8, 512, 192], P('district', 'sub')
- reservoir_duals: float32 [16, 48], replicated
Inputs may be any that keep to these rules, and one draw needn't show every extreme that they name: `neighbours`: each entry lies within 16 of its own balanced position and differs from it. `relayout`: each row is a permutation; of the subsystems at geographic positions s * 64 to (s + 1) * 64 - 1, exactly 8 go to balanced positions j * 64 to (j + 1) * 64 - 1, for every s and j. `ownership`: values of 16 or more mean that the subsystem draws from no reservoir.
All inputs are finite; a program needn't handle non-finite values.
Results may differ from a plain program's by a relative error of at most 0.018.
Values may be sent and summed in bfloat16 or wider, within the bound.
A program may use at most 64 MiB of HBM per device.

v0:
```python
import functools
import math

import jax
import jax.numpy as jnp
from jax import lax
from jax.experimental import pallas as pl
from jax.experimental.pallas import tpu as pltpu
from jax.sharding import PartitionSpec as P

REACH_SPAN = 16
LINK_COUNT = 4
RESERVOIRS = 16
OUTER_ITERS = 2
INNER_ITERS = 4
HALO = 2 * REACH_SPAN
LANES = 128

price_step = 0.3
reserve_step = 1.0

F32 = jnp.float32
BF16 = jnp.bfloat16
MESH = pl.DeviceIdType.MESH


def each(count, body):
    if count <= 8:
        for index in range(count):
            body(index)
    else:
        lax.fori_loop(0, count, lambda index, carry: (body(index), carry)[1], 0)


def mm(a, b):
    return jnp.dot(a, b, preferred_element_type=F32)


def contract(a, b, dim):
    return lax.dot_general(a, b, (((dim,), (dim,)), ((), ())), preferred_element_type=F32)


def kernel(
    dual_scale, costs_ref, meta_ref, relayout_ref, capacity_ref, coupling_hbm, factor_hbm,
    plan_ref, prices_ref, duals_ref,
    coupling, factor, meta, links, owners, gathered, base, state, flow, total, spread, weight,
    match, match_t, select, own_links, duals, draws, arrived,
    local_sem, meta_send, meta_recv, flow_send, flow_recv, draw_send, draw_recv,
):
    districts, rows, unknowns = costs_ref.shape
    interface = coupling.shape[2]
    horizon = capacity_ref.shape[1]
    group = relayout_ref.shape[1]
    sub_count = lax.axis_size("sub")
    district_count = lax.axis_size("district")
    me = lax.axis_index("sub")
    my_district = lax.axis_index("district")
    block = 2 * rows
    window = block + 2 * HALO
    blocks = group // block

    loads = []
    for d in range(districts):
        loads.append(
            (
                pltpu.make_async_copy(factor_hbm.at[d], factor.at[d], local_sem.at[2 * d]),
                pltpu.make_async_copy(coupling_hbm.at[d], coupling.at[d], local_sem.at[2 * d + 1]),
            )
        )
        for load in loads[-1]:
            load.start()

    barrier = pltpu.get_barrier_semaphore()
    for step in range(1, sub_count):
        pl.semaphore_signal(
            barrier, inc=1, device_id={"sub": lax.rem(me + step, sub_count)}, device_id_type=MESH
        )
    for step in range(1, district_count):
        pl.semaphore_signal(
            barrier,
            inc=1,
            device_id={"district": lax.rem(my_district + step, district_count)},
            device_id_type=MESH,
        )

    mine = pl.ds(pl.multiple_of(me * rows, rows), rows)
    for d in range(districts):
        for load in loads[d]:
            load.wait()
        first_plan = -mm(costs_ref[d], factor[d])
        gathered[d, mine, :] = mm(first_plan.astype(BF16), coupling[d]).astype(BF16)

    pl.semaphore_wait(barrier, sub_count - 1 + district_count - 1)
    sends = []
    for step in range(1, sub_count):
        target = lax.rem(me + step, sub_count)
        sends.append(
            pltpu.make_async_remote_copy(
                src_ref=meta_ref,
                dst_ref=meta.at[me],
                send_sem=meta_send.at[step],
                recv_sem=meta_recv.at[me],
                device_id={"sub": target},
                device_id_type=MESH,
            )
        )
        sends[-1].start()
    for step in range(1, sub_count):
        target = lax.rem(me + step, sub_count)
        sends.append(
            pltpu.make_async_remote_copy(
                src_ref=gathered.at[:, mine, :],
                dst_ref=gathered.at[:, mine, :],
                send_sem=flow_send.at[step],
                recv_sem=flow_recv.at[me],
                device_id={"sub": target},
                device_id_type=MESH,
            )
        )
        sends[-1].start()

    for d in range(districts):
        narrow = mm(factor[d], coupling[d]).astype(BF16)
        weight[d] = (-contract(coupling[d], narrow, 0)).astype(BF16)

    wide = rows + 2 * HALO
    for d in range(districts):
        moved = meta_ref[(LINK_COUNT + 1) * districts + d : (LINK_COUNT + 1) * districts + d + 1, :]
        place = lax.broadcasted_iota(jnp.int32, (group, rows), 0)
        select[d] = jnp.where(place == moved, 1.0, 0.0).astype(F32).T.astype(BF16)
        column = lax.broadcasted_iota(jnp.int32, (wide, rows), 0)
        row = lax.broadcasted_iota(jnp.int32, (wide, rows), 1)
        table = jnp.where(column == row + HALO, 1.0, 0.0)
        for k in range(LINK_COUNT):
            link = meta_ref[LINK_COUNT * d + k : LINK_COUNT * d + k + 1, :] - (me * rows - HALO)
            table = table - jnp.where(column == link, 1.0 / LINK_COUNT, 0.0)
        own_links[d] = table.T.astype(BF16)

    duals[...] = jnp.zeros_like(duals)
    duals[:, :horizon] = capacity_ref[...]
    capacity = duals[...]
    flow[...] = jnp.zeros_like(flow)
    links[...] = jnp.full_like(links, -window * 4)

    meta[me] = meta_ref[...]
    for step in range(1, sub_count):
        source = lax.rem(me + step, sub_count)
        pltpu.make_async_remote_copy(
            src_ref=meta_ref,
            dst_ref=meta.at[source],
            send_sem=meta_send.at[step],
            recv_sem=meta_recv.at[source],
            device_id={"sub": source},
            device_id_type=MESH,
        ).wait_recv()
    for source in range(sub_count):
        piece = meta[source]
        links[:, HALO + source * rows : HALO + (source + 1) * rows] = piece[: LINK_COUNT * districts]
        owners[:, source * rows : (source + 1) * rows] = piece[
            LINK_COUNT * districts : (LINK_COUNT + 1) * districts
        ]
    for d in range(districts):
        own = owners[d : d + 1, :]
        hit = jnp.where(
            lax.broadcasted_iota(jnp.int32, (RESERVOIRS, group), 0) == own, 1.0, 0.0
        ).astype(F32)
        match_t[d] = hit.astype(BF16)
        match[d] = hit.T.astype(BF16)

        def build(b, d=d):
            start = b * block if isinstance(b, int) else pl.multiple_of(b * block, block)
            column = lax.broadcasted_iota(jnp.int32, (window, window), 0)
            row = lax.broadcasted_iota(jnp.int32, (window, window), 1)
            table = jnp.where(column == row, 1.0, 0.0)
            for k in range(LINK_COUNT):
                at = LINK_COUNT * d + k
                link = links[at : at + 1, pl.ds(start, window)] - (start - HALO)
                table = table - jnp.where(column == link, 1.0 / LINK_COUNT, 0.0)
            table = table.T.astype(BF16)
            spread[d, b] = mm(table[HALO : HALO + block], table).astype(BF16)

        each(blocks, build)

    for step in range(1, sub_count):
        source = lax.rem(me + step, sub_count)
        pltpu.make_async_remote_copy(
            src_ref=gathered.at[:, mine, :],
            dst_ref=gathered.at[:, pl.ds(pl.multiple_of(source * rows, rows), rows), :],
            send_sem=flow_send.at[step],
            recv_sem=flow_recv.at[source],
            device_id={"sub": source},
            device_id_type=MESH,
        ).wait_recv()

    def at_block(b, extra=0, size=block):
        return pl.ds(b * block + extra, size)

    for d in range(districts):
        def permute(b, d=d):
            place = lax.broadcasted_iota(jnp.int32, (block, group), 0) + b * block
            chosen = jnp.where(place == relayout_ref[d : d + 1, :], 1.0, 0.0).astype(BF16)
            moved = mm(chosen, gathered[d])
            base[d, at_block(b), :] = moved
            flow[d, at_block(b, HALO), :] = moved.astype(BF16)

        each(blocks, permute)

    own_window = pl.ds(pl.multiple_of(me * rows, rows), wide)
    for d in range(districts):
        total[d] = flow[d, own_window, :].astype(F32)

        def begin(b, d=d):
            state[d, at_block(b), :] = price_step * mm(spread[d, b], flow[d, at_block(b, 0, window), :])

        each(blocks, begin)

    def forward():
        for d in range(districts):
            def one(b, d=d):
                price = state[d, at_block(b), :].astype(BF16)
                flow[d, at_block(b, HALO), :] = (base[d, at_block(b), :] + mm(price, weight[d])).astype(BF16)

            each(blocks, one)
            total[d] += flow[d, own_window, :].astype(F32)

    def backward():
        for d in range(districts):
            def one(b, d=d):
                state[d, at_block(b), :] += price_step * mm(
                    spread[d, b], flow[d, at_block(b, 0, window), :]
                )

            each(blocks, one)

    def inner(step, carry):
        forward()
        backward()
        return carry

    def send_draws(outer):
        drawn = mm(match_t[0], flow[0, HALO : HALO + group, :])
        for d in range(1, districts):
            drawn = drawn + mm(match_t[d], flow[d, HALO : HALO + group, :])
        draws[outer] = drawn[:, :LANES]
        copies = []
        for step in range(1, district_count):
            copies.append(
                pltpu.make_async_remote_copy(
                    src_ref=draws.at[outer],
                    dst_ref=arrived.at[outer, step],
                    send_sem=draw_send.at[outer, step],
                    recv_sem=draw_recv.at[outer, step],
                    device_id={"district": lax.rem(my_district + step, district_count)},
                    device_id_type=MESH,
                )
            )
            copies[-1].start()
        return copies

    def take_draws(outer, copies):
        drawn = draws[outer]
        for step in range(1, district_count):
            copies[step - 1].wait()
            drawn = drawn + arrived[outer, step]
        lane = lax.broadcasted_iota(jnp.int32, drawn.shape, 1)
        return jnp.where(lane < horizon, (drawn - capacity) * dual_scale, 0.0)

    lax.fori_loop(1, INNER_ITERS - 1, inner, 0)
    forward()
    copies = send_draws(0)
    backward()
    moved = take_draws(0, copies)
    for outer in range(1, OUTER_ITERS):
        duals[...] = moved if outer == 1 else duals[...] + moved
        high = moved.astype(BF16)
        low = (moved - high.astype(F32)).astype(BF16)
        for d in range(districts):
            state[d, :, :LANES] += mm(match[d], high) + mm(match[d], low)
        lax.fori_loop(0, INNER_ITERS - 1, inner, 0)
        forward()
        copies = send_draws(outer)
        if outer < OUTER_ITERS - 1:
            backward()
        else:
            for d in range(districts):
                chosen = mm(select[d], state[d].astype(BF16)).astype(BF16)
                gradient = costs_ref[d].astype(F32) + contract(chosen, coupling[d], 1)
                plan_ref[d] = -mm(gradient.astype(BF16), factor[d])
                summed = total[d]
                high = summed.astype(BF16)
                low = (summed - high.astype(F32)).astype(BF16)
                prices_ref[d] = price_step * (mm(own_links[d], high) + mm(own_links[d], low))
        moved = take_draws(outer, copies)
    duals_ref[...] = (duals[...] + moved)[:, :horizon]
    for send in sends:
        send.wait_send()


def on_device(cost_terms, neighbours, relayout, ownership, capacity, coupling, solve_factor):
    districts, rows, unknowns = cost_terms.shape
    interface = coupling.shape[2]
    group = relayout.shape[1]
    sub_count = lax.axis_size("sub")
    district_count = lax.axis_size("district")
    load_count = districts * district_count * group // (2 * RESERVOIRS)
    dual_scale = reserve_step / math.sqrt(load_count)
    own_moves = lax.dynamic_slice_in_dim(relayout, lax.axis_index("sub") * rows, rows, 1)
    meta = jnp.concatenate(
        [neighbours.transpose(0, 2, 1).reshape(districts * LINK_COUNT, rows), ownership, own_moves], axis=0
    )
    meta = jnp.pad(meta, ((0, -meta.shape[0] % 8), (0, 0)))
    block = 2 * rows
    blocks = group // block
    window = block + 2 * HALO
    vmem = pl.BlockSpec(memory_space=pltpu.VMEM)
    hbm = pl.BlockSpec(memory_space=pl.ANY)
    dma = pltpu.SemaphoreType.DMA
    return pl.pallas_call(
        functools.partial(kernel, dual_scale),
        name="districts",
        out_shape=(
            jax.ShapeDtypeStruct((districts, rows, unknowns), F32),
            jax.ShapeDtypeStruct((districts, rows, interface), F32),
            jax.ShapeDtypeStruct(capacity.shape, F32),
        ),
        in_specs=[vmem, vmem, vmem, vmem, hbm, hbm],
        out_specs=(vmem, vmem, vmem),
        scratch_shapes=[
            pltpu.VMEM(coupling.shape, BF16),
            pltpu.VMEM(solve_factor.shape, BF16),
            pltpu.VMEM((sub_count,) + meta.shape, jnp.int32),
            pltpu.VMEM((districts * LINK_COUNT, group + 2 * HALO), jnp.int32),
            pltpu.VMEM((districts, group), jnp.int32),
            pltpu.VMEM((districts, group, interface), BF16),
            pltpu.VMEM((districts, group, interface), F32),
            pltpu.VMEM((districts, group, interface), F32),
            pltpu.VMEM((districts, group + 2 * HALO, interface), BF16),
            pltpu.VMEM((districts, rows + 2 * HALO, interface), F32),
            pltpu.VMEM((districts, blocks, block, window), BF16),
            pltpu.VMEM((districts, interface, interface), BF16),
            pltpu.VMEM((districts, group, RESERVOIRS), BF16),
            pltpu.VMEM((districts, RESERVOIRS, group), BF16),
            pltpu.VMEM((districts, rows, group), BF16),
            pltpu.VMEM((districts, rows, rows + 2 * HALO), BF16),
            pltpu.VMEM((RESERVOIRS, LANES), F32),
            pltpu.VMEM((OUTER_ITERS, RESERVOIRS, LANES), F32),
            pltpu.VMEM((OUTER_ITERS, district_count, RESERVOIRS, LANES), F32),
            dma((2 * districts,)),
            dma((sub_count,)),
            dma((sub_count,)),
            dma((sub_count,)),
            dma((sub_count,)),
            dma((OUTER_ITERS, district_count)),
            dma((OUTER_ITERS, district_count)),
        ],
        compiler_params=pltpu.CompilerParams(
            collective_id=0, has_side_effects=True, vmem_limit_bytes=60 * 1024 * 1024
        ),
    )(cost_terms, meta, relayout, capacity, coupling, solve_factor)


def solution(mesh):
    placed = (
        P("district", "sub", None),
        P("district", "sub", None),
        P("district", None),
        P("district", "sub"),
        P(),
        P("district", None, None),
        P("district", None, None),
    )
    return jax.shard_map(
        on_device,
        mesh=mesh,
        in_specs=placed,
        out_specs=(P("district", "sub", None), P("district", "sub", None), P()),
        check_vma=False,
    )
```

profile of v0, /device:TPU:0, one launch (start us, length us, event | category | flops | bytes accessed | tf_op | source)
XLA Modules:
  0.0 39.0 jit_solution(7823395385368454731)
XLA Ops:
  0.6 0.8 %constant_dynamic-slice_fusion = s32[2,64]{1,0:T(2,128)S(1)} fusion(s32[2,512]{1,0:T(2,128)} %relayout_ref.1, s32[]{:T(128)S(6)} %select_n.3), kind=kLoop, calls=%fused_computation.1 | loop fusion | bytes 1028 | tf_op jit(solution)/shard_map/dynamic_slice | solution.py:307
  1.4 0.7 %pad_add_fusion = s32[12,64]{1,0:T(8,128)S(1)} fusion(s32[2,64]{1,0:T(2,128)S(1)} %constant_dynamic-slice_fusion, s32[2,64]{1,0:T(2,128)} %param.10, s32[8,64]{1,0:T(8,128)} %bitcast.3), kind=kLoop, calls=%fused_computation | loop fusion | flops 1536 | bytes 6144 | tf_op jit(solution)/shard_map/concatenate | solution.py:308
  2.1 0.6 %pad.4.meta_ref = s32[16,64]{1,0:T(8,128)} pad(s32[12,64]{1,0:T(8,128)S(1)} %pad_add_fusion, s32[]{:T(128)} %constant.4.clone.1), padding=0_4x0_0 | pad | bytes 7172 | tf_op jit(solution)/shard_map/jit(_pad)/pad | solution.py:311
  2.7 2.2 %copy.10.coupling_hbm = bf16[2,768,192]{2,1,0:T(8,128)(2,1)} copy(bf16[2,768,192]{1,2,0:T(8,128)(2,1)} %param.12) | data formatting | bytes 1179648 | tf_op args[5]
  4.9 29.4 %districts.1 = (f32[2,64,768]{2,1,0:T(8,128)}, f32[2,64,192]{2,1,0:T(8,128)}, f32[16,48]{1,0:T(8,128)}) custom-call(bf16[2,64,768]{2,1,0:T(8,128)(2,1)} %costs_ref.1, s32[16,64]{1,0:T(8,128)} %pad.4.meta_ref, s32[2,512]{1,0:T(2,128)} %relayout_ref.1, f32[16,48]{1,0:T(8,128)} %capacity_ref.1, bf16[2,768,192]{2,1,0:T(8,128)(2,1)} %copy.10.coupling_hbm, ...), custom_call_target="tpu_custom_call" | custom-call | tf_op jit(solution)/shard_map/districts/pallas_call | solution.py:318
  34.4 1.8 %copy.14 = f32[2,64,768]{2,1,0:T(8,128)} copy(f32[2,64,768]{2,1,0:T(8,128)} %get-tuple-element.6) | data formatting | bytes 786432
  36.1 1.6 %copy.15 = f32[2,64,192]{2,1,0:T(8,128)} copy(f32[2,64,192]{2,1,0:T(8,128)} %get-tuple-element.7) | data formatting | bytes 196608
  37.7 1.3 %copy.16 = f32[16,48]{1,0:T(8,128)} copy(f32[16,48]{1,0:T(8,128)} %get-tuple-element.8) | data formatting | bytes 6144
where the time goes:
time: 39.8 us; the launch traced here: 39 us
  Pallas kernels  29.4 us (74%)
  local copies, waits for them, and re-layouts  8.21 us (21%)
  other arithmetic  0.71 us (2%)
  between operations  0.64 us (2%)
    pallas_call x1, Pallas kernels, on_device(): pl.pallas_call(functools.partial(kernel, dual_scale), name='districts', o...  29.4 us
    unnamed x4, local copies, waits for them, and re-layouts  6.85 us

commit v1 on v0

--- a/solution.py
+++ b/solution.py
@@ -41,14 +41,14 @@
 
 
 def kernel(
-    dual_scale, costs_ref, meta_ref, relayout_ref, capacity_ref, coupling_hbm, factor_hbm,
+    dual_scale, costs_ref, near_ref, owner_ref, relayout_ref, capacity_ref, coupling_hbm, factor_hbm,
     plan_ref, prices_ref, duals_ref,
-    coupling, factor, meta, links, owners, gathered, base, state, flow, total, spread, weight,
+    coupling, factor, near, owned, links, owners, gathered, base, state, flow, total, spread, weight,
     match, match_t, select, own_links, duals, draws, arrived,
-    local_sem, meta_send, meta_recv, flow_send, flow_recv, draw_send, draw_recv,
+    local_sem, near_send, near_recv, owner_send, owner_recv, flow_send, flow_recv, draw_send, draw_recv,
 ):
     districts, rows, unknowns = costs_ref.shape
-    interface = coupling.shape[2]
+    interface = coupling.shape[1]
     horizon = capacity_ref.shape[1]
     group = relayout_ref.shape[1]
     sub_count = lax.axis_size("sub")
@@ -88,23 +88,27 @@
         for load in loads[d]:
             load.wait()
         first_plan = -mm(costs_ref[d], factor[d])
-        gathered[d, mine, :] = mm(first_plan.astype(BF16), coupling[d]).astype(BF16)
+        gathered[d, mine, :] = contract(first_plan.astype(BF16), coupling[d], 1).astype(BF16)
 
     pl.semaphore_wait(barrier, sub_count - 1 + district_count - 1)
     sends = []
     for step in range(1, sub_count):
         target = lax.rem(me + step, sub_count)
-        sends.append(
-            pltpu.make_async_remote_copy(
-                src_ref=meta_ref,
-                dst_ref=meta.at[me],
-                send_sem=meta_send.at[step],
-                recv_sem=meta_recv.at[me],
-                device_id={"sub": target},
-                device_id_type=MESH,
+        for source_ref, place_ref, send_sem, recv_sem in (
+            (near_ref, near, near_send, near_recv),
+            (owner_ref, owned, owner_send, owner_recv),
+        ):
+            sends.append(
+                pltpu.make_async_remote_copy(
+                    src_ref=source_ref,
+                    dst_ref=place_ref.at[me],
+                    send_sem=send_sem.at[step],
+                    recv_sem=recv_sem.at[me],
+                    device_id={"sub": target},
+                    device_id_type=MESH,
+                )
             )
-        )
-        sends[-1].start()
+            sends[-1].start()
     for step in range(1, sub_count):
         target = lax.rem(me + step, sub_count)
         sends.append(
@@ -120,19 +124,27 @@
         sends[-1].start()
 
     for d in range(districts):
-        narrow = mm(factor[d], coupling[d]).astype(BF16)
-        weight[d] = (-contract(coupling[d], narrow, 0)).astype(BF16)
+        narrow = mm(coupling[d], factor[d]).astype(BF16)
+        weight[d] = (-contract(narrow, coupling[d], 1)).astype(BF16)
 
     wide = rows + 2 * HALO
     for d in range(districts):
-        moved = meta_ref[(LINK_COUNT + 1) * districts + d : (LINK_COUNT + 1) * districts + d + 1, :]
-        place = lax.broadcasted_iota(jnp.int32, (group, rows), 0)
-        select[d] = jnp.where(place == moved, 1.0, 0.0).astype(F32).T.astype(BF16)
+        pick = lax.broadcasted_iota(jnp.int32, (rows, group), 1) == (
+            lax.broadcasted_iota(jnp.int32, (rows, group), 0) + me * rows
+        )
+        pick = jnp.where(pick, 1.0, 0.0).astype(BF16)
+
+        def choose(b, d=d, pick=pick):
+            place = lax.broadcasted_iota(jnp.int32, (block, group), 0) + b * block
+            chosen = jnp.where(place == relayout_ref[d : d + 1, :], 1.0, 0.0).astype(BF16)
+            select[d, b] = contract(pick, chosen, 1).astype(BF16)
+
+        each(blocks, choose)
         column = lax.broadcasted_iota(jnp.int32, (wide, rows), 0)
         row = lax.broadcasted_iota(jnp.int32, (wide, rows), 1)
         table = jnp.where(column == row + HALO, 1.0, 0.0)
         for k in range(LINK_COUNT):
-            link = meta_ref[LINK_COUNT * d + k : LINK_COUNT * d + k + 1, :] - (me * rows - HALO)
+            link = near_ref[LINK_COUNT * d + k : LINK_COUNT * d + k + 1, :] - (me * rows - HALO)
             table = table - jnp.where(column == link, 1.0 / LINK_COUNT, 0.0)
         own_links[d] = table.T.astype(BF16)
 
@@ -142,23 +154,25 @@
     flow[...] = jnp.zeros_like(flow)
     links[...] = jnp.full_like(links, -window * 4)
 
-    meta[me] = meta_ref[...]
+    near[me] = near_ref[...]
+    owned[me] = owner_ref[...]
     for step in range(1, sub_count):
         source = lax.rem(me + step, sub_count)
-        pltpu.make_async_remote_copy(
-            src_ref=meta_ref,
-            dst_ref=meta.at[source],
-            send_sem=meta_send.at[step],
-            recv_sem=meta_recv.at[source],
-            device_id={"sub": source},
-            device_id_type=MESH,
-        ).wait_recv()
+        for source_ref, place_ref, send_sem, recv_sem in (
+            (near_ref, near, near_send, near_recv),
+            (owner_ref, owned, owner_send, owner_recv),
+        ):
+            pltpu.make_async_remote_copy(
+                src_ref=source_ref,
+                dst_ref=place_ref.at[source],
+                send_sem=send_sem.at[step],
+                recv_sem=recv_sem.at[source],
+                device_id={"sub": source},
+                device_id_type=MESH,
+            ).wait_recv()
     for source in range(sub_count):
-        piece = meta[source]
-        links[:, HALO + source * rows : HALO + (source + 1) * rows] = piece[: LINK_COUNT * districts]
-        owners[:, source * rows : (source + 1) * rows] = piece[
-            LINK_COUNT * districts : (LINK_COUNT + 1) * districts
-        ]
+        links[:, HALO + source * rows : HALO + (source + 1) * rows] = near[source]
+        owners[:, source * rows : (source + 1) * rows] = owned[source]
     for d in range(districts):
         own = owners[d : d + 1, :]
         hit = jnp.where(
@@ -283,8 +297,12 @@
             backward()
         else:
             for d in range(districts):
-                chosen = mm(select[d], state[d].astype(BF16)).astype(BF16)
-                gradient = costs_ref[d].astype(F32) + contract(chosen, coupling[d], 1)
+                price = state[d].astype(BF16)
+                chosen = mm(select[d, 0], price[:block])
+                for b in range(1, blocks):
+                    chosen = chosen + mm(select[d, b], price[b * block : (b + 1) * block])
+                chosen = chosen.astype(BF16)
+                gradient = costs_ref[d].astype(F32) + mm(chosen, coupling[d])
                 plan_ref[d] = -mm(gradient.astype(BF16), factor[d])
                 summed = total[d]
                 high = summed.astype(BF16)
@@ -296,6 +314,19 @@
         send.wait_send()
 
 
+def handover(plan_ref, prices_ref, duals_ref, plan_out, prices_out, duals_out, sem):
+    copies = [
+        pltpu.make_async_copy(source, target, sem.at[index])
+        for index, (source, target) in enumerate(
+            ((plan_ref, plan_out), (prices_ref, prices_out), (duals_ref, duals_out))
+        )
+    ]
+    for copy in copies:
+        copy.start()
+    for copy in copies:
+        copy.wait()
+
+
 def on_device(cost_terms, neighbours, relayout, ownership, capacity, coupling, solve_factor):
     districts, rows, unknowns = cost_terms.shape
     interface = coupling.shape[2]
@@ -304,18 +335,15 @@
     district_count = lax.axis_size("district")
     load_count = districts * district_count * group // (2 * RESERVOIRS)
     dual_scale = reserve_step / math.sqrt(load_count)
-    own_moves = lax.dynamic_slice_in_dim(relayout, lax.axis_index("sub") * rows, rows, 1)
-    meta = jnp.concatenate(
-        [neighbours.transpose(0, 2, 1).reshape(districts * LINK_COUNT, rows), ownership, own_moves], axis=0
-    )
-    meta = jnp.pad(meta, ((0, -meta.shape[0] % 8), (0, 0)))
+    near = neighbours.transpose(0, 2, 1).reshape(districts * LINK_COUNT, rows)
+    coupling = coupling.transpose(0, 2, 1)
     block = 2 * rows
     blocks = group // block
     window = block + 2 * HALO
     vmem = pl.BlockSpec(memory_space=pltpu.VMEM)
     hbm = pl.BlockSpec(memory_space=pl.ANY)
     dma = pltpu.SemaphoreType.DMA
-    return pl.pallas_call(
+    results = pl.pallas_call(
         functools.partial(kernel, dual_scale),
         name="districts",
         out_shape=(
@@ -323,12 +351,13 @@
             jax.ShapeDtypeStruct((districts, rows, interface), F32),
             jax.ShapeDtypeStruct(capacity.shape, F32),
         ),
-        in_specs=[vmem, vmem, vmem, vmem, hbm, hbm],
+        in_specs=[vmem, vmem, vmem, vmem, vmem, hbm, hbm],
         out_specs=(vmem, vmem, vmem),
         scratch_shapes=[
             pltpu.VMEM(coupling.shape, BF16),
             pltpu.VMEM(solve_factor.shape, BF16),
-            pltpu.VMEM((sub_count,) + meta.shape, jnp.int32),
+            pltpu.VMEM((sub_count,) + near.shape, jnp.int32),
+            pltpu.VMEM((sub_count,) + ownership.shape, jnp.int32),
             pltpu.VMEM((districts * LINK_COUNT, group + 2 * HALO), jnp.int32),
             pltpu.VMEM((districts, group), jnp.int32),
             pltpu.VMEM((districts, group, interface), BF16),
@@ -340,7 +369,7 @@
             pltpu.VMEM((districts, interface, interface), BF16),
             pltpu.VMEM((districts, group, RESERVOIRS), BF16),
             pltpu.VMEM((districts, RESERVOIRS, group), BF16),
-            pltpu.VMEM((districts, rows, group), BF16),
+            pltpu.VMEM((districts, blocks, rows, block), BF16),
             pltpu.VMEM((districts, rows, rows + 2 * HALO), BF16),
             pltpu.VMEM((RESERVOIRS, LANES), F32),
             pltpu.VMEM((OUTER_ITERS, RESERVOIRS, LANES), F32),
@@ -350,13 +379,24 @@
             dma((sub_count,)),
             dma((sub_count,)),
             dma((sub_count,)),
+            dma((sub_count,)),
+            dma((sub_count,)),
             dma((OUTER_ITERS, district_count)),
             dma((OUTER_ITERS, district_count)),
         ],
         compiler_params=pltpu.CompilerParams(
-            collective_id=0, has_side_effects=True, vmem_limit_bytes=60 * 1024 * 1024
+            collective_id=0, has_side_effects=True, vmem_limit_bytes=(20 if group <= 1024 else 60) * 1024 * 1024
         ),
-    )(cost_terms, meta, relayout, capacity, coupling, solve_factor)
+    )(cost_terms, near, ownership, relayout, capacity, coupling, solve_factor)
+    return pl.pallas_call(
+        handover,
+        name="handover",
+        out_shape=tuple(jax.ShapeDtypeStruct(value.shape, value.dtype) for value in results),
+        in_specs=[hbm] * 3,
+        out_specs=(hbm,) * 3,
+        scratch_shapes=[dma((3,))],
+        compiler_params=pltpu.CompilerParams(vmem_limit_bytes=4 * 1024 * 1024),
+    )(*results)
 
 
 def solution(mesh):

time: 39.8 us -> 36.3 us (0.912)
  the two profiles are of different devices: /device:TPU:0 before, /device:TPU:11 now
where the time goes in v1:
time: 36.3 us; the launch traced here: 35.9 us
  Pallas kernels  28.9 us (80%)
  local copies, waits for them, and re-layouts  6.4 us (18%)
  between operations  0.66 us (2%)
    pallas_call x1, Pallas kernels, on_device(): pl.pallas_call(functools.partial(kernel, dual_scale), name='districts', o...  28 us
    unnamed x14, local copies, waits for them, and re-layouts  6.4 us
    pallas_call x1, Pallas kernels, on_device(): pl.pallas_call(handover, name='handover', out_shape=tuple((jax.ShapeDtype...  0.82 us

profile of v1, /device:TPU:11, one launch (start us, length us, event | category | flops | bytes accessed | tf_op | source)
XLA Modules:
  0.0 35.9 jit_solution(3047564787181344581)
XLA Ops:
  0.6 0.0 copy-start
  0.6 1.7 %copy-done = bf16[2,768,768]{2,1,0:T(8,128)(2,1)S(1)} copy-done((bf16[2,768,768]{2,1,0:T(8,128)(2,1)S(1)}, bf16[2,768,768]{2,1,0:T(8,128)(2,1)}, u32[]{:S(2)}) %copy-start) | copy-done | bytes 2359320
  2.3 0.0 copy-start.1
  2.3 1.1 %copy-done.1 = bf16[2,768,192]{1,2,0:T(8,128)(2,1)S(1)} copy-done((bf16[2,768,192]{1,2,0:T(8,128)(2,1)S(1)}, bf16[2,768,192]{1,2,0:T(8,128)(2,1)}, u32[]{:S(2)}) %copy-start.1) | copy-done | bytes 589848
  3.4 0.0 copy-start.2
  3.4 0.9 %copy-done.2 = bf16[2,64,768]{2,1,0:T(8,128)(2,1)S(1)} copy-done((bf16[2,64,768]{2,1,0:T(8,128)(2,1)S(1)}, bf16[2,64,768]{2,1,0:T(8,128)(2,1)}, u32[]{:S(2)}) %copy-start.2) | copy-done | bytes 196632
  4.3 0.0 copy-start.3
  4.3 0.7 %copy-done.3 = f32[16,48]{1,0:T(8,128)S(1)} copy-done((f32[16,48]{1,0:T(8,128)S(1)}, f32[16,48]{1,0:T(8,128)}, u32[]{:S(2)}) %copy-start.3) | copy-done | bytes 3096
  5.0 0.0 copy-start.4
  5.0 0.7 %copy-done.4 = s32[2,64,4]{1,2,0:T(4,128)S(1)} copy-done((s32[2,64,4]{1,2,0:T(4,128)S(1)}, s32[2,64,4]{1,2,0:T(4,128)}, u32[]{:S(2)}) %copy-start.4) | copy-done | bytes 2072
  5.7 0.0 copy-start.5
  5.7 0.7 %copy-done.5 = s32[2,512]{1,0:T(2,128)S(1)} copy-done((s32[2,512]{1,0:T(2,128)S(1)}, s32[2,512]{1,0:T(2,128)}, u32[]{:S(2)}) %copy-start.5) | copy-done | bytes 4120
  6.4 0.0 copy-start.6
  6.4 0.7 %copy-done.6 = s32[2,64]{1,0:T(2,128)S(1)} copy-done((s32[2,64]{1,0:T(2,128)S(1)}, s32[2,64]{1,0:T(2,128)}, u32[]{:S(2)}) %copy-start.6) | copy-done | bytes 536
  7.0 28.0 %districts.1 = (f32[2,64,768]{2,1,0:T(8,128)S(1)}, f32[2,64,192]{2,1,0:T(8,128)S(1)}, f32[16,48]{1,0:T(8,128)S(1)}) custom-call(bf16[2,64,768]{2,1,0:T(8,128)(2,1)S(1)} %copy-done.2, s32[8,64]{1,0:T(8,128)S(1)} %bitcast.5, s32[2,64]{1,0:T(2,128)S(1)} %copy-done.6, s32[2,512]{1,0:T(2,128)S(1)} %copy-done.5, f32[16,48]{1,0:T(8,128)S(1)} %copy-done.3, ...), custom_call_target="tpu_custom_call" | custom-call | tf_op jit(solution)/shard_map/districts/pallas_call | solution.py:346
  35.1 0.8 %handover.1 = (f32[2,64,768]{2,1,0:T(8,128)}, f32[2,64,192]{2,1,0:T(8,128)}, f32[16,48]{1,0:T(8,128)}) custom-call(f32[2,64,768]{2,1,0:T(8,128)S(1)} %get-tuple-element.6.plan_ref, f32[2,64,192]{2,1,0:T(8,128)S(1)} %get-tuple-element.7.prices_ref, f32[16,48]{1,0:T(8,128)S(1)} %get-tuple-element.8.duals_ref), custom_call_target="tpu_custom_call" | custom-call | tf_op jit(solution)/shard_map/handover/pallas_call | solution.py:391
Async XLA Ops:
  0.6 1.7 %copy-start = (bf16[2,768,768]{2,1,0:T(8,128)(2,1)S(1)}, bf16[2,768,768]{2,1,0:T(8,128)(2,1)}, u32[]{:S(2)}) copy-start(bf16[2,768,768]{2,1,0:T(8,128)(2,1)} %factor_hbm.1) | copy-start | bytes 7077892
  2.3 1.1 %copy-start.1 = (bf16[2,768,192]{1,2,0:T(8,128)(2,1)S(1)}, bf16[2,768,192]{1,2,0:T(8,128)(2,1)}, u32[]{:S(2)}) copy-start(bf16[2,768,192]{1,2,0:T(8,128)(2,1)} %param.12) | copy-start | bytes 1769476
  3.4 0.9 %copy-start.2 = (bf16[2,64,768]{2,1,0:T(8,128)(2,1)S(1)}, bf16[2,64,768]{2,1,0:T(8,128)(2,1)}, u32[]{:S(2)}) copy-start(bf16[2,64,768]{2,1,0:T(8,128)(2,1)} %costs_ref.1) | copy-start | bytes 589828
  4.3 0.7 %copy-start.3 = (f32[16,48]{1,0:T(8,128)S(1)}, f32[16,48]{1,0:T(8,128)}, u32[]{:S(2)}) copy-start(f32[16,48]{1,0:T(8,128)} %capacity_ref.1) | copy-start | bytes 9220
  5.0 0.7 %copy-start.4 = (s32[2,64,4]{1,2,0:T(4,128)S(1)}, s32[2,64,4]{1,2,0:T(4,128)}, u32[]{:S(2)}) copy-start(s32[2,64,4]{1,2,0:T(4,128)} %param.8) | copy-start | bytes 6148
  5.7 0.7 %copy-start.5 = (s32[2,512]{1,0:T(2,128)S(1)}, s32[2,512]{1,0:T(2,128)}, u32[]{:S(2)}) copy-start(s32[2,512]{1,0:T(2,128)} %relayout_ref.1) | copy-start | bytes 12292
  6.4 0.7 %copy-start.6 = (s32[2,64]{1,0:T(2,128)S(1)}, s32[2,64]{1,0:T(2,128)}, u32[]{:S(2)}) copy-start(s32[2,64]{1,0:T(2,128)} %owner_ref.1) | copy-start | bytes 1540

commit v2 on v1

--- a/solution.py
+++ b/solution.py
@@ -41,9 +41,9 @@
 
 
 def kernel(
-    dual_scale, costs_ref, near_ref, owner_ref, relayout_ref, capacity_ref, coupling_hbm, factor_hbm,
+    dual_scale, costs_hbm, near_hbm, owner_hbm, relayout_hbm, capacity_hbm, coupling_hbm, factor_hbm,
     plan_ref, prices_ref, duals_ref,
-    coupling, factor, near, owned, links, owners, gathered, base, state, flow, total, spread, weight,
+    costs_ref, near_ref, owner_ref, relayout_ref, capacity_ref, coupling, factor, near, owned, links, owners, gathered, base, state, flow, total, spread, weight,
     match, match_t, select, own_links, duals, draws, arrived,
     local_sem, near_send, near_recv, owner_send, owner_recv, flow_send, flow_recv, draw_send, draw_recv,
 ):
@@ -59,6 +59,8 @@
     window = block + 2 * HALO
     blocks = group // block
 
+    costs_load = pltpu.make_async_copy(costs_hbm, costs_ref, local_sem.at[2 * districts])
+    costs_load.start()
     loads = []
     for d in range(districts):
         loads.append(
@@ -69,6 +71,20 @@
         )
         for load in loads[-1]:
             load.start()
+
+    small_loads = [
+        pltpu.make_async_copy(source, target, local_sem.at[2 * districts + 1 + index])
+        for index, (source, target) in enumerate(
+            (
+                (near_hbm, near_ref),
+                (owner_hbm, owner_ref),
+                (relayout_hbm, relayout_ref),
+                (capacity_hbm, capacity_ref),
+            )
+        )
+    ]
+    for load in small_loads:
+        load.start()
 
     barrier = pltpu.get_barrier_semaphore()
     for step in range(1, sub_count):
@@ -83,6 +99,7 @@
             device_id_type=MESH,
         )
 
+    costs_load.wait()
     mine = pl.ds(pl.multiple_of(me * rows, rows), rows)
     for d in range(districts):
         for load in loads[d]:
@@ -90,6 +107,8 @@
         first_plan = -mm(costs_ref[d], factor[d])
         gathered[d, mine, :] = contract(first_plan.astype(BF16), coupling[d], 1).astype(BF16)
 
+    for load in small_loads:
+        load.wait()
     pl.semaphore_wait(barrier, sub_count - 1 + district_count - 1)
     sends = []
     for step in range(1, sub_count):
@@ -351,9 +370,14 @@
             jax.ShapeDtypeStruct((districts, rows, interface), F32),
             jax.ShapeDtypeStruct(capacity.shape, F32),
         ),
-        in_specs=[vmem, vmem, vmem, vmem, vmem, hbm, hbm],
+        in_specs=[pl.BlockSpec(memory_space=pltpu.HBM)] * 7,
         out_specs=(vmem, vmem, vmem),
         scratch_shapes=[
+            pltpu.VMEM(cost_terms.shape, BF16),
+            pltpu.VMEM(near.shape, jnp.int32),
+            pltpu.VMEM(ownership.shape, jnp.int32),
+            pltpu.VMEM(relayout.shape, jnp.int32),
+            pltpu.VMEM(capacity.shape, F32),
             pltpu.VMEM(coupling.shape, BF16),
             pltpu.VMEM(solve_factor.shape, BF16),
             pltpu.VMEM((sub_count,) + near.shape, jnp.int32),
@@ -374,7 +398,7 @@
             pltpu.VMEM((RESERVOIRS, LANES), F32),
             pltpu.VMEM((OUTER_ITERS, RESERVOIRS, LANES), F32),
             pltpu.VMEM((OUTER_ITERS, district_count, RESERVOIRS, LANES), F32),
-            dma((2 * districts,)),
+            dma((2 * districts + 5,)),
             dma((sub_count,)),
             dma((sub_count,)),
             dma((sub_count,)),
@@ -387,7 +411,7 @@
         compiler_params=pltpu.CompilerParams(
             collective_id=0, has_side_effects=True, vmem_limit_bytes=(20 if group <= 1024 else 60) * 1024 * 1024
         ),
-    )(cost_terms, near, ownership, relayout, capacity, coupling, solve_factor)
+    )(*[pltpu.with_memory_space_constraint(value, pltpu.HBM) for value in (cost_terms, near, ownership, relayout, capacity, coupling, solve_factor)])
     return pl.pallas_call(
         handover,
         name="handover",

time: 36.3 us -> 29.5 us (0.81)
  the two profiles are of different devices: /device:TPU:11 before, /device:TPU:9 now
where the time goes in v2:
time: 29.5 us; the launch traced here: 29.4 us
  Pallas kernels  28.7 us (97%)
  between operations  0.64 us (2%)
    pallas_call x1, Pallas kernels, on_device(): pl.pallas_call(functools.partial(kernel, dual_scale), name='districts', o...  27.9 us
    pallas_call x1, Pallas kernels, on_device(): pl.pallas_call(handover, name='handover', out_shape=tuple((jax.ShapeDtype...  0.82 us

profile of v2, /device:TPU:9, one launch (start us, length us, event | category | flops | bytes accessed | tf_op | source)
XLA Modules:
  0.0 29.4 jit_solution(16397530256946200556)
XLA Ops:
  0.6 27.9 %districts.1 = (f32[2,64,768]{2,1,0:T(8,128)S(1)}, f32[2,64,192]{2,1,0:T(8,128)S(1)}, f32[16,48]{1,0:T(8,128)S(1)}) custom-call(bf16[2,64,768]{2,1,0:T(8,128)(2,1)} %costs_hbm.1, s32[8,64]{1,0:T(8,128)} %bitcast.5, s32[2,64]{1,0:T(2,128)} %owner_hbm.1, s32[2,512]{1,0:T(2,128)} %relayout_hbm.1, f32[16,48]{1,0:T(8,128)} %capacity_hbm.1, ...), custom_call_target="tpu_custom_call" | custom-call | tf_op jit(solution)/shard_map/districts/pallas_call | solution.py:365
  28.6 0.8 %handover.1 = (f32[2,64,768]{2,1,0:T(8,128)}, f32[2,64,192]{2,1,0:T(8,128)}, f32[16,48]{1,0:T(8,128)}) custom-call(f32[2,64,768]{2,1,0:T(8,128)S(1)} %get-tuple-element.6.plan_ref, f32[2,64,192]{2,1,0:T(8,128)S(1)} %get-tuple-element.7.prices_ref, f32[16,48]{1,0:T(8,128)S(1)} %get-tuple-element.8.duals_ref), custom_call_target="tpu_custom_call" | custom-call | tf_op jit(solution)/shard_map/handover/pallas_call | solution.py:415

commit v3 on v2

v3 whole, which is shorter than its diff:
```python
import functools
import math

import jax
import jax.numpy as jnp
from jax import lax
from jax.experimental import pallas as pl
from jax.experimental.pallas import tpu as pltpu
from jax.sharding import PartitionSpec as P

REACH_SPAN = 16
LINK_COUNT = 4
RESERVOIRS = 16
OUTER_ITERS = 2
INNER_ITERS = 4
HALO = 2 * REACH_SPAN
LANES = 128

price_step = 0.3
reserve_step = 1.0

F32 = jnp.float32
BF16 = jnp.bfloat16
MESH = pl.DeviceIdType.MESH


def each(count, body):
    if count <= 8:
        for index in range(count):
            body(index)
    else:
        lax.fori_loop(0, count, lambda index, carry: (body(index), carry)[1], 0)


def mm(a, b):
    return jnp.dot(a, b, preferred_element_type=F32)


def contract(a, b, dim):
    return lax.dot_general(a, b, (((dim,), (dim,)), ((), ())), preferred_element_type=F32)


def kernel(
    dual_scale, costs_hbm, near_hbm, owner_hbm, relayout_hbm, capacity_hbm, coupling_hbm, factor_hbm,
    plan_ref, prices_ref, duals_ref,
    costs_ref, near_ref, owner_ref, relayout_ref, capacity_ref, coupling, factor, near, owned, links, owners, first, gathered, base, state, flow, total, spread, weight,
    match, match_t, select, near_links, chosen_out, chosen_in, prices_out, prices_in, duals, draws, arrived,
    local_sem, near_send, near_recv, owner_send, owner_recv, flow_send, flow_recv, draw_send, draw_recv,
    price_send, price_recv, dual_send, dual_recv,
):
    districts, rows, unknowns = costs_ref.shape
    interface = coupling.shape[1]
    horizon = capacity_ref.shape[1]
    group = relayout_ref.shape[1]
    sub_count = lax.axis_size("sub")
    district_count = lax.axis_size("district")
    me = lax.axis_index("sub")
    role = lax.rem(me, districts)
    team = me // districts * districts
    my_district = lax.axis_index("district")
    block = districts * rows
    window = block + 2 * HALO
    blocks = group // block

    costs_load = pltpu.make_async_copy(costs_hbm, costs_ref, local_sem.at[2 * districts])
    costs_load.start()
    loads = []
    for d in range(districts):
        loads.append(
            (
                pltpu.make_async_copy(factor_hbm.at[d], factor.at[d], local_sem.at[2 * d]),
                pltpu.make_async_copy(coupling_hbm.at[d], coupling.at[d], local_sem.at[2 * d + 1]),
            )
        )
        for load in loads[-1]:
            load.start()

    small_loads = [
        pltpu.make_async_copy(source, target, local_sem.at[2 * districts + 1 + index])
        for index, (source, target) in enumerate(
            (
                (near_hbm, near_ref),
                (owner_hbm, owner_ref),
                (relayout_hbm, relayout_ref),
                (capacity_hbm, capacity_ref),
            )
        )
    ]
    for load in small_loads:
        load.start()

    barrier = pltpu.get_barrier_semaphore()
    for step in range(1, sub_count):
        pl.semaphore_signal(
            barrier, inc=1, device_id={"sub": lax.rem(me + step, sub_count)}, device_id_type=MESH
        )
    for step in range(1, district_count):
        for other in range(districts):
            pl.semaphore_signal(
                barrier,
                inc=1,
                device_id={
                    "district": lax.rem(my_district + step, district_count),
                    "sub": team + lax.rem(role + other, districts),
                },
                device_id_type=MESH,
            )

    costs_load.wait()
    mine = pl.ds(pl.multiple_of(me * rows, rows), rows)
    for d in range(districts):
        for load in loads[d]:
            load.wait()
        first_plan = -mm(costs_ref[d], factor[d])
        first[d] = contract(first_plan.astype(BF16), coupling[d], 1).astype(BF16)

    for load in small_loads:
        load.wait()
    pl.semaphore_wait(barrier, sub_count - 1 + (district_count - 1) * districts)
    sends = []
    for step in range(1, sub_count):
        target = lax.rem(me + step, sub_count)
        for source_ref, place_ref, send_sem, recv_sem in (
            (near_ref, near, near_send, near_recv),
            (owner_ref, owned, owner_send, owner_recv),
        ):
            sends.append(
                pltpu.make_async_remote_copy(
                    src_ref=source_ref,
                    dst_ref=place_ref.at[me],
                    send_sem=send_sem.at[step],
                    recv_sem=recv_sem.at[me],
                    device_id={"sub": target},
                    device_id_type=MESH,
                )
            )
            sends[-1].start()
    for step in range(1, sub_count):
        target = lax.rem(me + step, sub_count)
        sends.append(
            pltpu.make_async_remote_copy(
                src_ref=first.at[lax.rem(target, districts)],
                dst_ref=gathered.at[mine, :],
                send_sem=flow_send.at[step],
                recv_sem=flow_recv.at[me],
                device_id={"sub": target},
                device_id_type=MESH,
            )
        )
        sends[-1].start()

    gathered[mine, :] = first[role]
    narrow = mm(coupling[role], factor[role]).astype(BF16)
    weight[...] = (-contract(narrow, coupling[role], 1)).astype(BF16)

    wide = rows + 2 * HALO
    moves = relayout_ref[pl.ds(role, 1), :]
    team_rows = districts * rows
    pick = lax.broadcasted_iota(jnp.int32, (team_rows, group), 1) == (
        lax.broadcasted_iota(jnp.int32, (team_rows, group), 0) + team * rows
    )
    pick = jnp.where(pick, 1.0, 0.0).astype(BF16)

    def choose(b):
        place = lax.broadcasted_iota(jnp.int32, (block, group), 0) + b * block
        chosen = jnp.where(place == moves, 1.0, 0.0).astype(BF16)
        select[b] = contract(pick, chosen, 1).astype(BF16)

    each(blocks, choose)

    duals[...] = jnp.zeros_like(duals)
    duals[:, :horizon] = capacity_ref[...]
    capacity = duals[...]
    flow[...] = jnp.zeros_like(flow)
    links[...] = jnp.full_like(links, -window * 4)

    near[me] = near_ref[...]
    owned[me] = owner_ref[...]
    for step in range(1, sub_count):
        source = lax.rem(me + step, sub_count)
        for source_ref, place_ref, send_sem, recv_sem in (
            (near_ref, near, near_send, near_recv),
            (owner_ref, owned, owner_send, owner_recv),
        ):
            pltpu.make_async_remote_copy(
                src_ref=source_ref,
                dst_ref=place_ref.at[source],
                send_sem=send_sem.at[step],
                recv_sem=recv_sem.at[source],
                device_id={"sub": source},
                device_id_type=MESH,
            ).wait_recv()
    for source in range(sub_count):
        links[:, HALO + source * rows : HALO + (source + 1) * rows] = near[source]
        owners[:, source * rows : (source + 1) * rows] = owned[source]
    own = owners[pl.ds(role, 1), :]
    hit = jnp.where(
        lax.broadcasted_iota(jnp.int32, (RESERVOIRS, group), 0) == own, 1.0, 0.0
    ).astype(F32)
    match_t[...] = hit.astype(BF16)
    match[...] = hit.T.astype(BF16)

    def linked(start, width):
        column = lax.broadcasted_iota(jnp.int32, (width, width), 0)
        row = lax.broadcasted_iota(jnp.int32, (width, width), 1)
        table = jnp.where(column == row, 1.0, 0.0)
        for k in range(LINK_COUNT):
            link = links[pl.ds(role * LINK_COUNT + k, 1), pl.ds(start, width)] - (start - HALO)
            table = table - jnp.where(column == link, 1.0 / LINK_COUNT, 0.0)
        return table.T.astype(BF16)

    def build(b):
        start = b * block if isinstance(b, int) else pl.multiple_of(b * block, block)
        table = linked(start, window)
        spread[b] = mm(table[HALO : HALO + block], table).astype(BF16)

    each(blocks, build)
    near_links[...] = linked(pl.multiple_of(team * rows, team_rows), window)[HALO : HALO + team_rows]

    for step in range(1, sub_count):
        source = lax.rem(me + step, sub_count)
        pltpu.make_async_remote_copy(
            src_ref=first.at[role],
            dst_ref=gathered.at[pl.ds(pl.multiple_of(source * rows, rows), rows), :],
            send_sem=flow_send.at[step],
            recv_sem=flow_recv.at[source],
            device_id={"sub": source},
            device_id_type=MESH,
        ).wait_recv()

    def at_block(b, extra=0, size=block):
        return pl.ds(b * block + extra, size)

    def permute(b):
        place = lax.broadcasted_iota(jnp.int32, (block, group), 0) + b * block
        chosen = jnp.where(place == moves, 1.0, 0.0).astype(BF16)
        moved = mm(chosen, gathered[...])
        base[at_block(b), :] = moved
        flow[at_block(b, HALO), :] = moved.astype(BF16)

    each(blocks, permute)

    team_window = pl.ds(pl.multiple_of(team * rows, team_rows), window)
    total[...] = flow[team_window, :].astype(F32)

    def begin(b):
        state[at_block(b), :] = price_step * mm(spread[b], flow[at_block(b, 0, window), :])

    each(blocks, begin)

    def forward():
        def one(b):
            price = state[at_block(b), :].astype(BF16)
            flow[at_block(b, HALO), :] = (base[at_block(b), :] + mm(price, weight[...])).astype(BF16)

        each(blocks, one)
        total[...] += flow[team_window, :].astype(F32)

    def backward():
        def one(b):
            state[at_block(b), :] += price_step * mm(spread[b], flow[at_block(b, 0, window), :])

        each(blocks, one)

    def inner(step, carry):
        forward()
        backward()
        return carry

    partners = [
        (step, other)
        for step in range(district_count)
        for other in range(districts)
        if step or other
    ]

    def partner(step, other):
        return {
            "district": lax.rem(my_district + step, district_count),
            "sub": team + lax.rem(role + other, districts),
        }

    def send_draws(outer):
        drawn = mm(match_t[...], flow[HALO : HALO + group, :])
        draws[outer] = drawn[:, :LANES]
        copies = []
        for index, (step, other) in enumerate(partners):
            copies.append(
                pltpu.make_async_remote_copy(
                    src_ref=draws.at[outer],
                    dst_ref=arrived.at[outer, index],
                    send_sem=draw_send.at[outer, index],
                    recv_sem=draw_recv.at[outer, index],
                    device_id=partner(step, other),
                    device_id_type=MESH,
                )
            )
            copies[-1].start()
        return copies

    def take_draws(outer, copies):
        drawn = draws[outer]
        for index, copy in enumerate(copies):
            copy.wait()
            drawn = drawn + arrived[outer, index]
        lane = lax.broadcasted_iota(jnp.int32, drawn.shape, 1)
        return jnp.where(lane < horizon, (drawn - capacity) * dual_scale, 0.0)

    def to_team(source_ref, place_ref, send_sem, recv_sem):
        copies = []
        for other in range(1, districts):
            target = lax.rem(role + other, districts)
            copies.append(
                pltpu.make_async_remote_copy(
                    src_ref=source_ref.at[target],
                    dst_ref=place_ref.at[role],
                    send_sem=send_sem.at[other],
                    recv_sem=recv_sem.at[other],
                    device_id={"sub": team + target},
                    device_id_type=MESH,
                )
            )
            copies[-1].start()
        return copies

    lax.fori_loop(1, INNER_ITERS - 1, inner, 0)
    forward()
    copies = send_draws(0)
    backward()
    moved = take_draws(0, copies)
    for outer in range(1, OUTER_ITERS):
        duals[...] = moved if outer == 1 else duals[...] + moved
        high = moved.astype(BF16)
        low = (moved - high.astype(F32)).astype(BF16)
        state[:, :LANES] += mm(match[...], high) + mm(match[...], low)
        lax.fori_loop(0, INNER_ITERS - 1, inner, 0)
        if outer == OUTER_ITERS - 1:
            price = state[...].astype(BF16)
            chosen = mm(select[0], price[:block])
            for b in range(1, blocks):
                chosen = chosen + mm(select[b], price[b * block : (b + 1) * block])
            chosen_out[...] = chosen.reshape(districts, rows, -1).astype(BF16)
            price_copies = to_team(chosen_out, chosen_in, price_send, price_recv)
            chosen_in[role] = chosen_out[role]
        forward()
        copies = send_draws(outer)
        if outer < OUTER_ITERS - 1:
            backward()
        else:
            high = total[...].astype(BF16)
            low = (total[...] - high.astype(F32)).astype(BF16)
            prices = price_step * (mm(near_links[...], high) + mm(near_links[...], low))
            prices_out[...] = prices.reshape(districts, rows, -1)
            dual_copies = to_team(prices_out, prices_in, dual_send, dual_recv)
            prices_in[role] = prices_out[role]
            for copy in price_copies:
                copy.wait()
            for d in range(districts):
                gradient = costs_ref[d].astype(F32) + mm(chosen_in[d], coupling[d])
                plan_ref[d] = -mm(gradient.astype(BF16), factor[d])
            for copy in dual_copies:
                copy.wait()
            prices_ref[...] = prices_in[...]
        moved = take_draws(outer, copies)
    duals_ref[...] = (duals[...] + moved)[:, :horizon]
    for send in sends:
        send.wait_send()


def handover(plan_ref, prices_ref, duals_ref, plan_out, prices_out, duals_out, sem):
    copies = [
        pltpu.make_async_copy(source, target, sem.at[index])
        for index, (source, target) in enumerate(
            ((plan_ref, plan_out), (prices_ref, prices_out), (duals_ref, duals_out))
        )
    ]
    for copy in copies:
        copy.start()
    for copy in copies:
        copy.wait()


def on_device(cost_terms, neighbours, relayout, ownership, capacity, coupling, solve_factor):
    districts, rows, unknowns = cost_terms.shape
    interface = coupling.shape[2]
    group = relayout.shape[1]
    sub_count = lax.axis_size("sub")
    district_count = lax.axis_size("district")
    load_count = districts * district_count * group // (2 * RESERVOIRS)
    dual_scale = reserve_step / math.sqrt(load_count)
    near = neighbours.transpose(0, 2, 1).reshape(districts * LINK_COUNT, rows)
    coupling = coupling.transpose(0, 2, 1)
    block = districts * rows
    blocks = group // block
    window = block + 2 * HALO
    vmem = pl.BlockSpec(memory_space=pltpu.VMEM)
    hbm = pl.BlockSpec(memory_space=pl.ANY)
    dma = pltpu.SemaphoreType.DMA
    results = pl.pallas_call(
        functools.partial(kernel, dual_scale),
        name="districts",
        out_shape=(
            jax.ShapeDtypeStruct((districts, rows, unknowns), F32),
            jax.ShapeDtypeStruct((districts, rows, interface), F32),
            jax.ShapeDtypeStruct(capacity.shape, F32),
        ),
        in_specs=[pl.BlockSpec(memory_space=pltpu.HBM)] * 7,
        out_specs=(vmem, vmem, vmem),
        scratch_shapes=[
            pltpu.VMEM(cost_terms.shape, BF16),
            pltpu.VMEM(near.shape, jnp.int32),
            pltpu.VMEM(ownership.shape, jnp.int32),
            pltpu.VMEM(relayout.shape, jnp.int32),
            pltpu.VMEM(capacity.shape, F32),
            pltpu.VMEM(coupling.shape, BF16),
            pltpu.VMEM(solve_factor.shape, BF16),
            pltpu.VMEM((sub_count,) + near.shape, jnp.int32),
            pltpu.VMEM((sub_count,) + ownership.shape, jnp.int32),
            pltpu.VMEM((districts * LINK_COUNT, group + 2 * HALO), jnp.int32),
            pltpu.VMEM((districts, group), jnp.int32),
            pltpu.VMEM((districts, rows, interface), BF16),
            pltpu.VMEM((group, interface), BF16),
            pltpu.VMEM((group, interface), F32),
            pltpu.VMEM((group, interface), F32),
            pltpu.VMEM((group + 2 * HALO, interface), BF16),
            pltpu.VMEM((window, interface), F32),
            pltpu.VMEM((blocks, block, window), BF16),
            pltpu.VMEM((interface, interface), BF16),
            pltpu.VMEM((group, RESERVOIRS), BF16),
            pltpu.VMEM((RESERVOIRS, group), BF16),
            pltpu.VMEM((blocks, block, block), BF16),
            pltpu.VMEM((block, window), BF16),
            pltpu.VMEM((districts, rows, interface), BF16),
            pltpu.VMEM((districts, rows, interface), BF16),
            pltpu.VMEM((districts, rows, interface), F32),
            pltpu.VMEM((districts, rows, interface), F32),
            pltpu.VMEM((RESERVOIRS, LANES), F32),
            pltpu.VMEM((OUTER_ITERS, RESERVOIRS, LANES), F32),
            pltpu.VMEM((OUTER_ITERS, district_count * districts, RESERVOIRS, LANES), F32),
            dma((2 * districts + 5,)),
            dma((sub_count,)),
            dma((sub_count,)),
            dma((sub_count,)),
            dma((sub_count,)),
            dma((sub_count,)),
            dma((sub_count,)),
            dma((OUTER_ITERS, district_count * districts)),
            dma((OUTER_ITERS, district_count * districts)),
            dma((districts,)),
            dma((districts,)),
            dma((districts,)),
            dma((districts,)),
        ],
        compiler_params=pltpu.CompilerParams(
            collective_id=0, has_side_effects=True, vmem_limit_bytes=(20 if group <= 1024 else 60) * 1024 * 1024
        ),
    )(*[pltpu.with_memory_space_constraint(value, pltpu.HBM) for value in (cost_terms, near, ownership, relayout, capacity, coupling, solve_factor)])
    return pl.pallas_call(
        handover,
        name="handover",
        out_shape=tuple(jax.ShapeDtypeStruct(value.shape, value.dtype) for value in results),
        in_specs=[hbm] * 3,
        out_specs=(hbm,) * 3,
        scratch_shapes=[dma((3,))],
        compiler_params=pltpu.CompilerParams(vmem_limit_bytes=4 * 1024 * 1024),
    )(*results)


def solution(mesh):
    placed = (
        P("district", "sub", None),
        P("district", "sub", None),
        P("district", None),
        P("district", "sub"),
        P(),
        P("district", None, None),
        P("district", None, None),
    )
    return jax.shard_map(
        on_device,
        mesh=mesh,
        in_specs=placed,
        out_specs=(P("district", "sub", None), P("district", "sub", None), P()),
        check_vma=False,
    )
```

time: 29.5 us -> 28.1 us (0.953)
  the two profiles are of different devices: /device:TPU:9 before, /device:TPU:0 now
where the time goes in v3:
time: 28.1 us; the launch traced here: 27.9 us
  Pallas kernels  27.3 us (97%)
  between operations  0.64 us (2%)
    pallas_call x1, Pallas kernels, on_device(): pl.pallas_call(functools.partial(kernel, dual_scale), name='districts', o...  26.5 us
    pallas_call x1, Pallas kernels, on_device(): pl.pallas_call(handover, name='handover', out_shape=tuple((jax.ShapeDtype...  0.82 us

profile of v3, /device:TPU:0, one launch (start us, length us, event | category | flops | bytes accessed | tf_op | source)
XLA Modules:
  0.0 27.9 jit_solution(3648082301845855318)
XLA Ops:
  0.6 26.5 %districts.1 = (f32[2,64,768]{2,1,0:T(8,128)S(1)}, f32[2,64,192]{2,1,0:T(8,128)S(1)}, f32[16,48]{1,0:T(8,128)S(1)}) custom-call(bf16[2,64,768]{2,1,0:T(8,128)(2,1)} %costs_hbm.1, s32[8,64]{1,0:T(8,128)} %bitcast.5, s32[2,64]{1,0:T(2,128)} %owner_hbm.1, s32[2,512]{1,0:T(2,128)} %relayout_hbm.1, f32[16,48]{1,0:T(8,128)} %capacity_hbm.1, ...), custom_call_target="tpu_custom_call" | custom-call | tf_op jit(solution)/shard_map/districts/pallas_call | solution.py:399
  27.1 0.8 %handover.1 = (f32[2,64,768]{2,1,0:T(8,128)}, f32[2,64,192]{2,1,0:T(8,128)}, f32[16,48]{1,0:T(8,128)}) custom-call(f32[2,64,768]{2,1,0:T(8,128)S(1)} %get-tuple-element.6.plan_ref, f32[2,64,192]{2,1,0:T(8,128)S(1)} %get-tuple-element.7.prices_ref, f32[16,48]{1,0:T(8,128)S(1)} %get-tuple-element.8.duals_ref), custom_call_target="tpu_custom_call" | custom-call | tf_op jit(solution)/shard_map/handover/pallas_call | solution.py:458

commit v4 on v3

--- a/solution.py
+++ b/solution.py
@@ -135,7 +135,7 @@
                 )
             )
             sends[-1].start()
-    for step in range(1, sub_count):
+    for step in sorted(range(1, sub_count), key=lambda step: abs(2 * step - sub_count)):
         target = lax.rem(me + step, sub_count)
         sends.append(
             pltpu.make_async_remote_copy(

time: 28.1 us -> 28.7 us (1.021)
  Pallas kernels: 27.3 us -> 27.9 us
    pallas_call x1, Pallas kernels: 26.5 us -> 27.1 us  [on_device(): pl.pallas_call(functools.partial(kernel, dual_scale), name='districts', o...]
where the time goes in v4:
time: 28.7 us; the launch traced here: 28.6 us
  Pallas kernels  27.9 us (97%)
  between operations  0.64 us (2%)
    pallas_call x1, Pallas kernels, on_device(): pl.pallas_call(functools.partial(kernel, dual_scale), name='districts', o...  27.1 us
    pallas_call x1, Pallas kernels, on_device(): pl.pallas_call(handover, name='handover', out_shape=tuple((jax.ShapeDtype...  0.82 us

profile of v4, /device:TPU:0, one launch (start us, length us, event | category | flops | bytes accessed | tf_op | source)
XLA Modules:
  0.0 28.6 jit_solution(12410182947045400799)
XLA Ops:
  0.6 27.1 %districts.1 = (f32[2,64,768]{2,1,0:T(8,128)S(1)}, f32[2,64,192]{2,1,0:T(8,128)S(1)}, f32[16,48]{1,0:T(8,128)S(1)}) custom-call(bf16[2,64,768]{2,1,0:T(8,128)(2,1)} %costs_hbm.1, s32[8,64]{1,0:T(8,128)} %bitcast.5, s32[2,64]{1,0:T(2,128)} %owner_hbm.1, s32[2,512]{1,0:T(2,128)} %relayout_hbm.1, f32[16,48]{1,0:T(8,128)} %capacity_hbm.1, ...), custom_call_target="tpu_custom_call" | custom-call | tf_op jit(solution)/shard_map/districts/pallas_call | solution.py:399
  27.7 0.8 %handover.1 = (f32[2,64,768]{2,1,0:T(8,128)}, f32[2,64,192]{2,1,0:T(8,128)}, f32[16,48]{1,0:T(8,128)}) custom-call(f32[2,64,768]{2,1,0:T(8,128)S(1)} %get-tuple-element.6.plan_ref, f32[2,64,192]{2,1,0:T(8,128)S(1)} %get-tuple-element.7.prices_ref, f32[16,48]{1,0:T(8,128)S(1)} %get-tuple-element.8.duals_ref), custom_call_target="tpu_custom_call" | custom-call | tf_op jit(solution)/shard_map/handover/pallas_call | solution.py:458
